TPU v7x, 32 devices: a whole 2x2x4 slice. The times are simulated.
32 devices in a mesh: row: 8 (over z, core), col: 4 (over y, x).
Axes of the slice: x: 2, y: 2, z: 4, core: 2. Of those that a mesh axis runs over, the one named last changes fastest.
Arguments:
- tensor: bfloat16 [512, 2048, 256], P(('row', 'col')), may hold values from -6 to 6
- factor_one: bfloat16 [512, 64], P(('row', 'col')), may hold values from -0.25 to 0.25
- factor_two: bfloat16 [2048, 64], P('col'), may hold values from -0.125 to 0.125
Outputs:
- gram: float32 [256, 256], replicated
All inputs are finite; a program needn't handle non-finite values.
Results may differ from a plain program's by a relative error of at most 0.0003.
Values may be sent and summed in bfloat16 or wider, within the bound.
A program may use at most 64 MiB of HBM per device.

v0:
```python
import jax
import jax.numpy as jnp
from jax import lax
from jax.sharding import PartitionSpec as P

R1 = 64
R2 = 64


def apply_first(partly, first):
    return jnp.einsum(
        "ark,as->srk", partly, first.astype(jnp.float32), precision=lax.Precision.HIGHEST
    )


def per_device(tensor, factor_one, factor_two):
    whole_two = lax.all_gather(factor_two, "col", axis=0, tiled=True)
    partly = jnp.einsum("abk,br->ark", tensor, whole_two, preferred_element_type=jnp.float32)
    scale = R1 * R2
    partial_core = apply_first(partly, factor_one)
    flat_part = partial_core.reshape(R1 * R2, partial_core.shape[2])
    summed = lax.psum(flat_part, ("row", "col"))
    gram = jnp.dot(
        summed.T, summed, precision=lax.Precision.HIGHEST, preferred_element_type=jnp.float32
    )
    return gram / scale


def solution(mesh):
    placed = (P(("row", "col"), None, None), P(("row", "col"), None), P("col", None))
    return jax.shard_map(per_device, mesh=mesh, in_specs=placed, out_specs=P(), check_vma=False)
```

profile of v0, /device:TPU:0, one launch (start us, length us, event | category | flops | bytes accessed | tf_op | source)
XLA Modules:
  0.0 193.5 jit_solution(18068110036583877398)
XLA Ops:
  6.5 0.0 copy-start
  6.5 0.0 all-reduce.2.cloned.1.call-start
  6.5 10.9 %all_gather.3 = bf16[2048,64]{0,1:T(8,128)(2,1)S(1)} all-gather(bf16[512,64]{0,1:T(8,128)(2,1)} %param.5), channel_id=1, replica_groups=mesh['row'=8,'col'=4] {'col'}, dimensions={0}, use_global_device_ids=true | all-gather | bytes 327680 | tf_op jit(solution)/shard_map/all_gather | solution.py:17
  17.4 8.7 %fusion.2 = f32[64,16,256]{2,0,1:T(8,128)S(1)} fusion(bf16[16,2048,256]{2,1,0:T(8,128)(2,1)} %param.3, bf16[2048,64]{0,1:T(8,128)(2,1)S(1)} %all_gather.3), kind=kOutput, calls=%fused_computation.4 | convolution fusion | flops 1073741824 | bytes 18087936 | tf_op jit(solution)/shard_map/abk,br->ark/dot_general | solution.py:18
  26.2 0.0 copy-done
  26.2 2.1 %convolution_bitcast_fusion = f32[64,64,256]{2,0,1:T(8,128)S(1)} fusion(f32[64,16,256]{2,0,1:T(8,128)S(1)} %fusion.2, bf16[16,64]{1,0:T(8,128)(2,1)S(1)} %copy-done), kind=kOutput, calls=%fused_computation | convolution fusion | flops 201326592 | bytes 5244928 | tf_op jit(solution)/shard_map/ark,as->srk/dot_general | solution.py:11
  28.3 4.4 %copy.4 = f32[64,64,256]{2,1,0:T(8,128)} copy(f32[64,64,256]{2,0,1:T(8,128)S(1)} %convolution_bitcast_fusion) | data formatting | bytes 8388608 | tf_op jit(solution)/shard_map/ark,as->srk/dot_general | solution.py:11
  32.7 0.0 all-reduce.2.cloned.1.call-update
  32.7 143.0 %all-reduce.2.cloned.1.call-done = f32[4096,256]{1,0:T(8,128)} async-done(((f32[4096,256]{1,0:T(8,128)}), f32[4096,256]{1,0:T(8,128)}) %all-reduce.2.cloned.1.call-update) | async-done | bytes 4194320 | tf_op jit(solution)/shard_map/psum | solution.py:22
  175.7 10.9 %convolution_multiply_fusion = f32[256,256]{1,0:T(8,128)} fusion(f32[4096,256]{1,0:T(8,128)} %all-reduce.2.cloned.1.call-done), kind=kOutput, calls=%fused_computation.1 | convolution fusion | flops 3221291008 | bytes 4456448 | tf_op jit(solution)/shard_map/dot_general | solution.py:23
Async XLA Ops:
  6.5 19.6 %copy-start = (bf16[16,64]{1,0:T(8,128)(2,1)S(1)}, bf16[16,64]{1,0:T(8,128)(2,1)}, u32[]{:S(2)}) copy-start(bf16[16,64]{1,0:T(8,128)(2,1)} %param.4) | copy-start | bytes 6148
  6.5 169.2 %all-reduce.2.cloned.1.call-start = ((), (), s32[]{:S(2)}) async-start(), calls=%async_computation | async-start | bytes 8388608 | tf_op jit(solution)/shard_map/psum | solution.py:22
Sparse Core Ops, SparseCore 0:
  32.8 142.8 all-reduce.1
where the time goes:
time: 194 us; the launch traced here: 193 us
  waiting for transfers between devices  143 us (74%)
  matrix products  21.8 us (11%)
  between operations  13.4 us (7%)
  blocking collectives  10.9 us (6%)
  local copies, waits for them, and re-layouts  4.39 us (2%)
    psum x1, waiting for transfers between devices, per_device(): summed = lax.psum(flat_part, ('row', 'col'))  143 us
    dot_general x1, matrix products, per_device(): jnp.dot(summed.T, summed, precision=lax.Precision.HIGHEST, preferred_elem...  10.9 us
    all_gather x1, blocking collectives, per_device(): whole_two = lax.all_gather(factor_two, 'col', axis=0, tiled=True)  10.9 us
    dot_general x1, matrix products, per_device(): jnp.einsum('abk,br->ark', tensor, whole_two, preferred_element_type=jnp.f...  8.75 us
    dot_general x1, local copies, waits for them, and re-layouts, apply_first(): jnp.einsum('ark,as->srk', partly, first.astype(jnp.float32), precision=la...  4.39 us
  transfers between devices with their start and end apart: 1, of which 1 were waited for; matrix products, arithmetic and copies ran while one was open for 0% of the time, Pallas kernels for 0%

commit v1 on v0

--- a/solution.py
+++ b/solution.py
@@ -7,6 +7,22 @@
 R2 = 64
 
 
+def product_in_turn(value, axis, dim, term):
+    size, index, width = (lax.axis_size(axis), lax.axis_index(axis), value.shape[dim])
+    right = [(i, (i + 1) % size) for i in range(size)]
+    left = [(i, (i - 1) % size) for i in range(size)]
+    middle = size // 2
+    from_left = from_right = value
+    total = term(value, index * width)
+    for step in range(1, middle + 1):
+        from_left = lax.ppermute(from_left, axis, right)
+        if step < size - middle:
+            from_right = lax.ppermute(from_right, axis, left)
+            total = total + term(from_right, (index + step) % size * width)
+        total = total + term(from_left, (index - step) % size * width)
+    return total
+
+
 def apply_first(partly, first):
     return jnp.einsum(
         "ark,as->srk", partly, first.astype(jnp.float32), precision=lax.Precision.HIGHEST
@@ -14,8 +30,17 @@
 
 
 def per_device(tensor, factor_one, factor_two):
-    whole_two = lax.all_gather(factor_two, "col", axis=0, tiled=True)
-    partly = jnp.einsum("abk,br->ark", tensor, whole_two, preferred_element_type=jnp.float32)
+    partly = product_in_turn(
+        factor_two,
+        "col",
+        0,
+        lambda own_block, at: jnp.einsum(
+            "abk,br->ark",
+            lax.dynamic_slice_in_dim(tensor, at, own_block.shape[0], axis=1),
+            own_block,
+            preferred_element_type=jnp.float32,
+        ),
+    )
     scale = R1 * R2
     partial_core = apply_first(partly, factor_one)
     flat_part = partial_core.reshape(R1 * R2, partial_core.shape[2])

time: 194 us -> 195 us (level)
  blocking collectives: 10.9 us -> 0 us
  matrix products: 21.8 us -> 28.1 us
  starting transfers between devices: 0.01 us -> 5.05 us
    all_gather x1 -> x0, blocking collectives: 10.9 us -> none  [per_device(): whole_two = lax.all_gather(factor_two, 'col', axis=0, tiled=True)]
    ppermute x0 -> x3, starting transfers between devices: none -> 5.04 us  [the longest x2 4.09 us: product_in_turn(): from_left = lax.ppermute(from_left, axis, right)]
    dot_general x1 -> x4, matrix products: 8.75 us -> 12.2 us  [per_device(): jnp.einsum('abk,br->ark', lax.dynamic_slice_in_dim(tensor, at, own_block....]
    dot_general x1, matrix products: 2.1 us -> 4.82 us  [apply_first(): jnp.einsum('ark,as->srk', partly, first.astype(jnp.float32), precision=la...]
  transfers between devices with their start and end apart: 1 -> 4, of which waited for: 1 -> 1; matrix products, arithmetic and copies ran while one was open for 0% -> 5% of each run, Pallas kernels for 0% -> 0%
where the time goes in v1:
time: 195 us
  waiting for transfers between devices  144 us (74%)
  matrix products  28.1 us (14%)
  between operations  13.5 us (7%)
  starting transfers between devices  5.05 us (3%)
  local copies, waits for them, and re-layouts  4.4 us (2%)
    psum x1, waiting for transfers between devices, per_device(): summed = lax.psum(flat_part, ('row', 'col'))  144 us
    dot_general x4, matrix products, per_device(): jnp.einsum('abk,br->ark', lax.dynamic_slice_in_dim(tensor, at, own_block....  12.2 us
    dot_general x1, matrix products, per_device(): jnp.dot(summed.T, summed, precision=lax.Precision.HIGHEST, preferred_elem...  11.1 us
    dot_general x1, matrix products, apply_first(): jnp.einsum('ark,as->srk', partly, first.astype(jnp.float32), precision=la...  4.82 us
    dot_general x1, local copies, waits for them, and re-layouts, apply_first(): jnp.einsum('ark,as->srk', partly, first.astype(jnp.float32), precision=la...  4.39 us
    ppermute x2, starting transfers between devices, product_in_turn(): from_left = lax.ppermute(from_left, axis, right)  4.09 us
  transfers between devices with their start and end apart: 4, of which 1 were waited for; matrix products, arithmetic and copies ran while one was open for 5% of the time, Pallas kernels for 0%

profile of v1, /device:TPU:0, one launch (start us, length us, event | category | flops | bytes accessed | tf_op | source)
XLA Modules:
  0.0 194.9 jit_solution(1353250398234768788)
XLA Ops:
  6.5 0.0 copy-start
  6.5 0.0 all-reduce.2.cloned.1.call-start
  6.5 3.0 %collective-permute-start.1 = (bf16[512,64]{0,1:T(8,128)(2,1)}, bf16[512,64]{0,1:T(8,128)(2,1)S(1)}, u32[]{:S(2)}, u32[]{:S(2)}) collective-permute-start(bf16[512,64]{0,1:T(8,128)(2,1)} %param.5), channel_id=1, source_target_pairs={{0,1},{1,2},{2,3},{3,0},{4,5},{5,6},{6,7},{7,4},{8,9},{9,10},{10,1... | collective-permute-start | bytes 196616 | tf_op jit(solution)/shard_map/ppermute | solution.py:18
  9.5 1.0 collective-permute-start
  10.5 3.1 %fusion.6 = f32[16,256,64]{1,2,0:T(8,128)S(1)} fusion(bf16[16,2048,256]{2,1,0:T(8,128)(2,1)} %param.3, s32[]{:T(128)S(6)} %select_n.27, bf16[512,64]{0,1:T(8,128)(2,1)} %param.5), kind=kOutput, calls=%fused_computation.6 | convolution fusion | flops 268435456 | bytes 5308420 | tf_op jit(solution)/shard_map/abk,br->ark/dot_general | solution.py:37
  13.6 0.0 collective-permute-done.1
  13.6 1.1 collective-permute-start.2
  14.7 3.0 %fusion.2 = f32[16,256,64]{1,2,0:T(8,128)S(1)} fusion(bf16[16,2048,256]{2,1,0:T(8,128)(2,1)} %param.3, s32[]{:T(128)S(6)} %select_n.31, bf16[512,64]{0,1:T(8,128)(2,1)S(1)} %collective-permute-done.1), kind=kOutput, calls=%fused_computation.2 | convolution fusion | flops 268435456 | bytes 5308420 | tf_op jit(solution)/shard_map/abk,br->ark/dot_general | solution.py:37
  17.8 0.0 collective-permute-done
  17.8 3.0 %fusion.4 = f32[16,256,64]{1,2,0:T(8,128)S(1)} fusion(bf16[16,2048,256]{2,1,0:T(8,128)(2,1)} %param.3, s32[]{:T(128)S(6)} %select_n.29, bf16[512,64]{0,1:T(8,128)(2,1)S(1)} %collective-permute-done), kind=kOutput, calls=%fused_computation.4 | convolution fusion | flops 268435456 | bytes 5308420 | tf_op jit(solution)/shard_map/abk,br->ark/dot_general | solution.py:37
  20.8 0.0 collective-permute-done.2
  20.8 3.0 %fusion = f32[16,256,64]{1,2,0:T(8,128)S(1)} fusion(bf16[16,2048,256]{2,1,0:T(8,128)(2,1)} %param.3, s32[]{:T(128)S(6)} %select_n.33, bf16[512,64]{0,1:T(8,128)(2,1)S(1)} %collective-permute-done.2), kind=kOutput, calls=%fused_computation | convolution fusion | flops 268435456 | bytes 5308420 | tf_op jit(solution)/shard_map/abk,br->ark/dot_general | solution.py:37
  23.9 0.0 copy-done
  23.9 4.8 %convolution_bitcast_fusion = f32[64,64,256]{2,0,1:T(8,128)S(1)} fusion(f32[16,256,64]{1,2,0:T(8,128)S(1)} %fusion, f32[16,256,64]{1,2,0:T(8,128)S(1)} %fusion.2, f32[16,256,64]{1,2,0:T(8,128)S(1)} %fusion.4, f32[16,256,64]{1,2,0:T(8,128)S(1)} %fusion.6, bf16[16,64]{1,0:T(8,128)(2,1)S(1)} %copy-done), kind=kOutput, calls=%fused_computation.8 | convolution fusion | flops 202113024 | bytes 8390656 | tf_op jit(solution)/shard_map/ark,as->srk/dot_general | solution.py:27
  28.7 4.4 %copy.4 = f32[64,64,256]{2,1,0:T(8,128)} copy(f32[64,64,256]{2,0,1:T(8,128)S(1)} %convolution_bitcast_fusion) | data formatting | bytes 8388608 | tf_op jit(solution)/shard_map/ark,as->srk/dot_general | solution.py:27
  33.1 0.0 all-reduce.2.cloned.1.call-update
  33.1 143.8 %all-reduce.2.cloned.1.call-done = f32[4096,256]{1,0:T(8,128)} async-done(((f32[4096,256]{1,0:T(8,128)}), f32[4096,256]{1,0:T(8,128)}) %all-reduce.2.cloned.1.call-update) | async-done | bytes 4194320 | tf_op jit(solution)/shard_map/psum | solution.py:47
  176.9 11.1 %convolution_multiply_fusion = f32[256,256]{1,0:T(8,128)} fusion(f32[4096,256]{1,0:T(8,128)} %all-reduce.2.cloned.1.call-done), kind=kOutput, calls=%fused_computation.9 | convolution fusion | flops 3221291008 | bytes 4456448 | tf_op jit(solution)/shard_map/dot_general | solution.py:48
Async XLA Ops:
  6.5 17.3 %copy-start = (bf16[16,64]{1,0:T(8,128)(2,1)S(1)}, bf16[16,64]{1,0:T(8,128)(2,1)}, u32[]{:S(2)}) copy-start(bf16[16,64]{1,0:T(8,128)(2,1)} %param.4) | copy-start | bytes 6148
  6.5 170.4 %all-reduce.2.cloned.1.call-start = ((), (), s32[]{:S(2)}) async-start(), calls=%async_computation | async-start | bytes 8388608 | tf_op jit(solution)/shard_map/psum | solution.py:47
  6.5 7.1 %collective-permute-start.1 = (bf16[512,64]{0,1:T(8,128)(2,1)}, bf16[512,64]{0,1:T(8,128)(2,1)S(1)}, u32[]{:S(2)}, u32[]{:S(2)}) collective-permute-start(bf16[512,64]{0,1:T(8,128)(2,1)} %param.5), channel_id=1, source_target_pairs={{0,1},{1,2},{2,3},{3,0},{4,5},{5,6},{6,7},{7,4},{8,9},{9,10},{10,1... | collective-permute-start | bytes 196616 | tf_op jit(solution)/shard_map/ppermute | solution.py:18
  9.5 8.3 %collective-permute-start = (bf16[512,64]{0,1:T(8,128)(2,1)}, bf16[512,64]{0,1:T(8,128)(2,1)S(1)}, u32[]{:S(2)}, u32[]{:S(2)}) collective-permute-start(bf16[512,64]{0,1:T(8,128)(2,1)} %param.5), channel_id=1, source_target_pairs={{0,3},{1,0},{2,1},{3,2},{4,7},{5,4},{6,5},{7,6},{8,11},{9,8},{10,9... | collective-permute-start | bytes 196616 | tf_op jit(solution)/shard_map/ppermute | solution.py:20
  13.6 7.2 %collective-permute-start.2 = (bf16[512,64]{0,1:T(8,128)(2,1)S(1)}, bf16[512,64]{0,1:T(8,128)(2,1)S(1)}, u32[]{:S(2)}, u32[]{:S(2)}) collective-permute-start(bf16[512,64]{0,1:T(8,128)(2,1)S(1)} %collective-permute-done.1), channel_id=1, source_target_pairs={{0,1},{1,2},{2,3},{3,0},{4,5},{5,6},{6,7},{7,4},{8,9},{9,10},{10,1... | collective-permute-start | bytes 196616 | tf_op jit(solution)/shard_map/ppermute | solution.py:18
Sparse Core Ops, SparseCore 0:
  33.2 143.6 all-reduce.1

commit v2 on v0

--- a/solution.py
+++ b/solution.py
@@ -14,7 +14,12 @@
 
 
 def per_device(tensor, factor_one, factor_two):
-    whole_two = lax.all_gather(factor_two, "col", axis=0, tiled=True)
+    ring = [factor_two]
+    for hop in range(3):
+        ring.append(lax.ppermute(ring[-1], "col", [(dev, (dev + 1) % 4) for dev in range(4)]))
+    whole_two = jnp.roll(
+        jnp.concatenate(ring[::-1], axis=0), (lax.axis_index("col") + 1) * ring[0].shape[0], axis=0
+    )
     partly = jnp.einsum("abk,br->ark", tensor, whole_two, preferred_element_type=jnp.float32)
     scale = R1 * R2
     partial_core = apply_first(partly, factor_one)

time: 194 us -> 202 us (1.041)
  waiting for transfers between devices: 143 us -> 156 us
  blocking collectives: 10.9 us -> 0 us
  starting transfers between devices: 0.01 us -> 4.24 us
    ppermute x0 -> x3, waiting for transfers between devices: none -> 12.5 us  [per_device(): lax.ppermute(ring[-1], 'col', [(dev, (dev + 1) % 4) for dev in range(4)])]
    all_gather x1 -> x0, blocking collectives: 10.9 us -> none  [per_device(): whole_two = lax.all_gather(factor_two, 'col', axis=0, tiled=True)]
    ppermute x0 -> x3, starting transfers between devices: none -> 4.23 us  [per_device(): lax.ppermute(ring[-1], 'col', [(dev, (dev + 1) % 4) for dev in range(4)])]
  transfers between devices with their start and end apart: 1 -> 4, of which waited for: 1 -> 4; matrix products, arithmetic and copies ran while one was open for 0% -> 0% of each run, Pallas kernels for 0% -> 0%
where the time goes in v2:
time: 202 us
  waiting for transfers between devices  156 us (77%)
  matrix products  21.8 us (11%)
  between operations  13.4 us (7%)
  local copies, waits for them, and re-layouts  6.13 us (3%)
  starting transfers between devices  4.24 us (2%)
    psum x1, waiting for transfers between devices, per_device(): summed = lax.psum(flat_part, ('row', 'col'))  143 us
    ppermute x3, waiting for transfers between devices, per_device(): lax.ppermute(ring[-1], 'col', [(dev, (dev + 1) % 4) for dev in range(4)])  12.5 us
    dot_general x1, matrix products, per_device(): jnp.dot(summed.T, summed, precision=lax.Precision.HIGHEST, preferred_elem...  10.9 us
    dot_general x1, matrix products, per_device(): jnp.einsum('abk,br->ark', tensor, whole_two, preferred_element_type=jnp.f...  8.75 us
    dot_general x1, local copies, waits for them, and re-layouts, apply_first(): jnp.einsum('ark,as->srk', partly, first.astype(jnp.float32), precision=la...  4.39 us
    ppermute x3, starting transfers between devices, per_device(): lax.ppermute(ring[-1], 'col', [(dev, (dev + 1) % 4) for dev in range(4)])  4.23 us
  transfers between devices with their start and end apart: 4, of which 4 were waited for; matrix products, arithmetic and copies ran while one was open for 0% of the time, Pallas kernels for 0%

profile of v2, /device:TPU:0, one launch (start us, length us, event | category | flops | bytes accessed | tf_op | source)
XLA Modules:
  0.0 201.5 jit_solution(16211037745078322438)
XLA Ops:
  6.5 0.0 copy-start
  6.5 0.0 all-reduce.2.cloned.1.call-start
  6.5 3.0 %collective-permute-start = (bf16[512,64]{0,1:T(8,128)(2,1)}, bf16[512,64]{0,1:T(8,128)(2,1)S(1)}, u32[]{:S(2)}, u32[]{:S(2)}) collective-permute-start(bf16[512,64]{0,1:T(8,128)(2,1)} %param.5), channel_id=1, source_target_pairs={{0,1},{1,2},{2,3},{3,0},{4,5},{5,6},{6,7},{7,4},{8,9},{9,10},{10,1... | collective-permute-start | bytes 196616 | tf_op jit(solution)/shard_map/ppermute | solution.py:19
  9.5 3.4 %collective-permute-done = bf16[512,64]{0,1:T(8,128)(2,1)S(1)} collective-permute-done((bf16[512,64]{0,1:T(8,128)(2,1)}, bf16[512,64]{0,1:T(8,128)(2,1)S(1)}, u32[]{:S(2)}, u32[]{:S(2)}) %collective-permute-start) | collective-permute-done | bytes 65568 | tf_op jit(solution)/shard_map/ppermute | solution.py:19
  12.9 1.1 collective-permute-start.1
  14.0 4.1 %collective-permute-done.1 = bf16[512,64]{0,1:T(8,128)(2,1)S(1)} collective-permute-done((bf16[512,64]{0,1:T(8,128)(2,1)S(1)}, bf16[512,64]{0,1:T(8,128)(2,1)S(1)}, u32[]{:S(2)}, u32[]{:S(2)}) %collective-permute-start.1) | collective-permute-done | bytes 65568 | tf_op jit(solution)/shard_map/ppermute | solution.py:19
  18.1 0.2 collective-permute-start.2
  18.3 5.0 %collective-permute-done.2 = bf16[512,64]{0,1:T(8,128)(2,1)S(1)} collective-permute-done((bf16[512,64]{0,1:T(8,128)(2,1)S(1)}, bf16[512,64]{0,1:T(8,128)(2,1)S(1)}, u32[]{:S(2)}, u32[]{:S(2)}) %collective-permute-start.2) | collective-permute-done | bytes 65568 | tf_op jit(solution)/shard_map/ppermute | solution.py:19
  23.3 0.8 constant_dynamic-update-slice_fusion.4
  24.2 0.8 constant_dynamic-update-slice_fusion
  25.0 8.7 %fusion.2 = f32[64,16,256]{2,0,1:T(8,128)S(1)} fusion(bf16[16,2048,256]{2,1,0:T(8,128)(2,1)} %param.3, bf16[4096,64]{0,1:T(8,128)(2,1)S(1)} %constant_dynamic-update-slice_fusion, s32[]{:T(128)S(6)} %select_n.14), kind=kOutput, calls=%fused_computation.4 | convolution fusion | flops 1073741824 | bytes 18087940 | tf_op jit(solution)/shard_map/abk,br->ark/dot_general | solution.py:23
  33.8 0.0 copy-done
  33.8 2.1 %convolution_bitcast_fusion = f32[64,64,256]{2,0,1:T(8,128)S(1)} fusion(f32[64,16,256]{2,0,1:T(8,128)S(1)} %fusion.2, bf16[16,64]{1,0:T(8,128)(2,1)S(1)} %copy-done), kind=kOutput, calls=%fused_computation | convolution fusion | flops 201326592 | bytes 5244928 | tf_op jit(solution)/shard_map/ark,as->srk/dot_general | solution.py:11
  35.9 4.4 %copy.4 = f32[64,64,256]{2,1,0:T(8,128)} copy(f32[64,64,256]{2,0,1:T(8,128)S(1)} %convolution_bitcast_fusion) | data formatting | bytes 8388608 | tf_op jit(solution)/shard_map/ark,as->srk/dot_general | solution.py:11
  40.3 0.0 all-reduce.2.cloned.1.call-update
  40.3 143.4 %all-reduce.2.cloned.1.call-done = f32[4096,256]{1,0:T(8,128)} async-done(((f32[4096,256]{1,0:T(8,128)}), f32[4096,256]{1,0:T(8,128)}) %all-reduce.2.cloned.1.call-update) | async-done | bytes 4194320 | tf_op jit(solution)/shard_map/psum | solution.py:27
  183.7 10.9 %convolution_multiply_fusion = f32[256,256]{1,0:T(8,128)} fusion(f32[4096,256]{1,0:T(8,128)} %all-reduce.2.cloned.1.call-done), kind=kOutput, calls=%fused_computation.1 | convolution fusion | flops 3221291008 | bytes 4456448 | tf_op jit(solution)/shard_map/dot_general | solution.py:28
  (6 shorter events, 0.0 us)
Async XLA Ops:
  6.5 27.2 %copy-start = (bf16[16,64]{1,0:T(8,128)(2,1)S(1)}, bf16[16,64]{1,0:T(8,128)(2,1)}, u32[]{:S(2)}) copy-start(bf16[16,64]{1,0:T(8,128)(2,1)} %param.4) | copy-start | bytes 6148
  6.5 177.2 %all-reduce.2.cloned.1.call-start = ((), (), s32[]{:S(2)}) async-start(), calls=%async_computation | async-start | bytes 8388608 | tf_op jit(solution)/shard_map/psum | solution.py:27
  6.5 6.4 %collective-permute-start = (bf16[512,64]{0,1:T(8,128)(2,1)}, bf16[512,64]{0,1:T(8,128)(2,1)S(1)}, u32[]{:S(2)}, u32[]{:S(2)}) collective-permute-start(bf16[512,64]{0,1:T(8,128)(2,1)} %param.5), channel_id=1, source_target_pairs={{0,1},{1,2},{2,3},{3,0},{4,5},{5,6},{6,7},{7,4},{8,9},{9,10},{10,1... | collective-permute-start | bytes 196616 | tf_op jit(solution)/shard_map/ppermute | solution.py:19
  12.9 5.2 %collective-permute-start.1 = (bf16[512,64]{0,1:T(8,128)(2,1)S(1)}, bf16[512,64]{0,1:T(8,128)(2,1)S(1)}, u32[]{:S(2)}, u32[]{:S(2)}) collective-permute-start(bf16[512,64]{0,1:T(8,128)(2,1)S(1)} %collective-permute-done), channel_id=1, source_target_pairs={{0,1},{1,2},{2,3},{3,0},{4,5},{5,6},{6,7},{7,4},{8,9},{9,10},{10,1... | collective-permute-start | bytes 196616 | tf_op jit(solution)/shard_map/ppermute | solution.py:19
  18.1 5.2 %collective-permute-start.2 = (bf16[512,64]{0,1:T(8,128)(2,1)S(1)}, bf16[512,64]{0,1:T(8,128)(2,1)S(1)}, u32[]{:S(2)}, u32[]{:S(2)}) collective-permute-start(bf16[512,64]{0,1:T(8,128)(2,1)S(1)} %collective-permute-done.1), channel_id=1, source_target_pairs={{0,1},{1,2},{2,3},{3,0},{4,5},{5,6},{6,7},{7,4},{8,9},{9,10},{10,1... | collective-permute-start | bytes 196616 | tf_op jit(solution)/shard_map/ppermute | solution.py:19
Sparse Core Ops, SparseCore 0:
  40.4 143.2 all-reduce.1

commit v3 on v0

--- a/solution.py
+++ b/solution.py
@@ -19,7 +19,7 @@
     scale = R1 * R2
     partial_core = apply_first(partly, factor_one)
     flat_part = partial_core.reshape(R1 * R2, partial_core.shape[2])
-    summed = lax.psum(flat_part, ("row", "col"))
+    summed = lax.psum(lax.psum(flat_part, "col"), "row")
     gram = jnp.dot(
         summed.T, summed, precision=lax.Precision.HIGHEST, preferred_element_type=jnp.float32
     )

time: 194 us -> 254 us (1.31)
  waiting for transfers between devices: 143 us -> 203 us
    psum x1 -> x2, waiting for transfers between devices: 143 us -> 203 us  [per_device(): summed = lax.psum(lax.psum(flat_part, 'col'), 'row')]
  transfers between devices with their start and end apart: 1 -> 2, of which waited for: 1 -> 2; matrix products, arithmetic and copies ran while one was open for 0% -> 0% of each run, Pallas kernels for 0% -> 0%
where the time goes in v3:
time: 254 us; the launch traced here: 253 us
  waiting for transfers between devices  203 us (80%)
  matrix products  21.8 us (9%)
  between operations  13.4 us (5%)
  blocking collectives  10.9 us (4%)
  local copies, waits for them, and re-layouts  4.39 us (2%)
    psum x2, waiting for transfers between devices, per_device(): summed = lax.psum(lax.psum(flat_part, 'col'), 'row')  203 us
    dot_general x1, matrix products, per_device(): jnp.dot(summed.T, summed, precision=lax.Precision.HIGHEST, preferred_elem...  10.9 us
    all_gather x1, blocking collectives, per_device(): whole_two = lax.all_gather(factor_two, 'col', axis=0, tiled=True)  10.9 us
    dot_general x1, matrix products, per_device(): jnp.einsum('abk,br->ark', tensor, whole_two, preferred_element_type=jnp.f...  8.75 us
  transfers between devices with their start and end apart: 2, of which 2 were waited for; matrix products, arithmetic and copies ran while one was open for 0% of the time, Pallas kernels for 0%

profile of v3, /device:TPU:0, one launch (start us, length us, event | category | flops | bytes accessed | tf_op | source)
XLA Modules:
  0.0 253.4 jit_solution(12762084684466608124)
XLA Ops:
  6.5 0.0 copy-start
  6.5 0.0 all-reduce.3.cloned.1.call-start
  6.5 10.9 %all_gather.3 = bf16[2048,64]{0,1:T(8,128)(2,1)S(1)} all-gather(bf16[512,64]{0,1:T(8,128)(2,1)} %param.5), channel_id=1, replica_groups=mesh['row'=8,'col'=4] {'col'}, dimensions={0}, use_global_device_ids=true | all-gather | bytes 327680 | tf_op jit(solution)/shard_map/all_gather | solution.py:17
  17.4 8.7 %fusion.2 = f32[64,16,256]{2,0,1:T(8,128)S(1)} fusion(bf16[16,2048,256]{2,1,0:T(8,128)(2,1)} %param.3, bf16[2048,64]{0,1:T(8,128)(2,1)S(1)} %all_gather.3), kind=kOutput, calls=%fused_computation.4 | convolution fusion | flops 1073741824 | bytes 18087936 | tf_op jit(solution)/shard_map/abk,br->ark/dot_general | solution.py:18
  26.2 0.0 copy-done
  26.2 2.1 convolution_bitcast_fusion
  28.3 4.4 %copy.4 = f32[64,64,256]{2,1,0:T(8,128)} copy(f32[64,64,256]{2,0,1:T(8,128)S(1)} %convolution_bitcast_fusion) | data formatting | bytes 8388608 | tf_op jit(solution)/shard_map/ark,as->srk/dot_general | solution.py:11
  32.7 0.0 all-reduce.3.cloned.1.call-update
  32.7 0.2 all-reduce.5.cloned.1.call-start
  32.9 103.8 %all-reduce.3.cloned.1.call-done = f32[4096,256]{1,0:T(8,128)} async-done(((f32[4096,256]{1,0:T(8,128)}), f32[4096,256]{1,0:T(8,128)}) %all-reduce.3.cloned.1.call-update) | async-done | bytes 4194320 | tf_op jit(solution)/shard_map/psum | solution.py:22
  136.7 0.0 all-reduce.5.cloned.1.call-update
  136.7 98.9 %all-reduce.5.cloned.1.call-done = f32[4096,256]{1,0:T(8,128)} async-done(((f32[4096,256]{1,0:T(8,128)}), f32[4096,256]{1,0:T(8,128)}) %all-reduce.5.cloned.1.call-update) | async-done | bytes 4194320 | tf_op jit(solution)/shard_map/psum | solution.py:22
  235.6 10.9 %convolution_multiply_fusion = f32[256,256]{1,0:T(8,128)} fusion(f32[4096,256]{1,0:T(8,128)} %all-reduce.5.cloned.1.call-done), kind=kOutput, calls=%fused_computation.1 | convolution fusion | flops 3221291008 | bytes 4456448 | tf_op jit(solution)/shard_map/dot_general | solution.py:23
Async XLA Ops:
  6.5 19.6 %copy-start = (bf16[16,64]{1,0:T(8,128)(2,1)S(1)}, bf16[16,64]{1,0:T(8,128)(2,1)}, u32[]{:S(2)}) copy-start(bf16[16,64]{1,0:T(8,128)(2,1)} %param.4) | copy-start | bytes 6148
  6.5 130.2 %all-reduce.3.cloned.1.call-start = ((), (), s32[]{:S(2)}) async-start(), calls=%async_computation | async-start | bytes 8388608 | tf_op jit(solution)/shard_map/psum | solution.py:22
  32.7 202.9 %all-reduce.5.cloned.1.call-start = ((), (), s32[]{:S(2)}) async-start(), calls=%async_computation.1 | async-start | bytes 8388608 | tf_op jit(solution)/shard_map/psum | solution.py:22
Sparse Core Ops, SparseCore 0:
  32.8 103.8 all-reduce.2
  139.1 96.4 all-reduce.4
